TPU v7x, 512 devices: a 4x2x32 block of a 4x16x32 slice. The times are simulated.
512 devices in a mesh: groups: 2 (over y), row: 32 (over z), col: 4 (over x), sub: 2 (over core).
Axes of the slice: x: 4, y: 2, z: 32, core: 2. Of those that a mesh axis runs over, the one named last changes fastest.
The devices are a block of a 4x16x32 slice.
Arguments:
- matrix: float32 [16384, 8192], P(('groups', 'row'), ('col', 'sub')), parts along dimension 0, may hold values from -60 to 60
- basis_vectors: float32 [16384, 1024], P(('groups', 'row'), ('col', 'sub')), parts along dimension 0, may hold values from -0.0625 to 0.0625
- split_size: int32 [2], P('groups'), parts along dimension 0, may hold values from 256 to 767
Outputs:
- children: float32 [2, 2048, 1024], P('sub', ('groups', 'row'), 'col'), parts along dimension 1
There are 2 independent parts, one for each index of `groups`. A program takes and returns all parts, laid end to end along the dimension named above; each array names one. Nothing has to cross between parts.
Inputs may be any that keep to these rules, and one draw needn't show every extreme that they name: The second subspace has 1024 minus split_size vectors.
All inputs are finite; a program needn't handle non-finite values.
Results may differ from a plain program's by a relative error of at most 0.00011.
Values sent between devices are 32-bit elements; how exact they have to be, the bound alone decides.
No kernel may reach another device: no remote copies, remote signals or barrier semaphores. Data moves between devices by JAX's collectives and lax.ppermute only.
A program may use at most 64 MiB of HBM per device.

v0:
```python
import jax
import jax.numpy as jnp
from jax import lax
from jax.sharding import PartitionSpec as P

PRECISION = lax.Precision.HIGHEST
NEAR = 4


def shifted(array, axis, step):
    size = lax.axis_size(axis)
    return lax.ppermute(array, axis, [(i, (i + step) % size) for i in range(size)])


def swapped(array, axis):
    size = lax.axis_size(axis)
    return lax.ppermute(array, axis, [(i, i ^ 1) for i in range(size)])


def product(left, right, contract):
    return lax.dot_general(
        left, right, (contract, ((), ())), precision=PRECISION, preferred_element_type=jnp.float32
    )


def all_columns(basis):
    half = basis.shape[0] // 2
    parts = [
        lax.all_gather(basis[i * half : (i + 1) * half], ("col", "sub"), axis=0) for i in range(2)
    ]
    return parts


def shards(matrix, basis_vectors, split_size):
    rows_here, width = matrix.shape
    n_row = lax.axis_size("row")
    n_col = lax.axis_size("col")
    row = lax.axis_index("row")
    col = lax.axis_index("col")
    sub = lax.axis_index("sub")
    parity = row % 2
    every_other = [[first + 2 * i for i in range(n_row // 2)] for first in range(2)]
    strip = lax.all_gather(basis_vectors, "row", axis=0, tiled=True, axis_index_groups=every_other)
    blocks = matrix.reshape(rows_here, width // (2 * rows_here), 2, rows_here)
    keep = jnp.where(parity == 0, blocks[:, :, 0], blocks[:, :, 1]).reshape(rows_here, width // 2)
    give = jnp.where(parity == 0, blocks[:, :, 1], blocks[:, :, 0]).reshape(rows_here, width // 2)
    own = jnp.concatenate([keep, swapped(give, "row")], axis=0)
    before = shifted(own, "col", 1)
    after = shifted(own, "col", -1)
    half = own.shape[0] // 2
    across = jnp.concatenate(
        [shifted(before[:half], "col", 1), shifted(after[half:], "col", -1)], axis=0
    )
    pieces = {0: own, 1: before, 2: across, 3: after}
    mate = swapped(basis_vectors, "row")
    pair_basis = jnp.concatenate(all_columns(basis_vectors) + all_columns(mate), axis=1)
    span = own.shape[1]
    image = None
    for distance, piece in pieces.items():
        source = (col - distance) % n_col
        other = swapped(piece, "sub")
        for core, operand in ((sub, piece), (1 - sub, other)):
            rows = lax.dynamic_slice_in_dim(strip, (source * 2 + core) * span, span, 0)
            part = product(operand, rows, ((1,), (0,)))
            image = part if image is None else image + part
    partial = product(pair_basis, image, ((1,), (0,)))
    total = partial.shape[0] * partial.shape[1]
    share = total // n_row
    far = n_row // NEAR
    partial = partial.reshape(far, NEAR, share, -1).swapaxes(0, 1)
    near_groups = [[NEAR * g + q for q in range(NEAR)] for g in range(far)]
    far_groups = [[NEAR * g + q for g in range(far)] for q in range(NEAR)]
    partial = lax.all_to_all(partial, "row", 0, 0, tiled=True, axis_index_groups=near_groups).sum(0)
    proj_block = lax.all_to_all(partial, "row", 0, 0, tiled=True, axis_index_groups=far_groups).sum(
        0
    )
    child_block = lax.all_gather(proj_block, "sub", axis=1, tiled=True)
    row_ids = jnp.arange(child_block.shape[0], dtype=jnp.int32) + row * child_block.shape[0]
    col_ids = jnp.arange(child_block.shape[1], dtype=jnp.int32) + col * child_block.shape[1]
    leading = split_size[0]
    row_first = row_ids < leading
    col_first = col_ids < leading
    mask_one = row_first[:, None] & col_first[None, :]
    mask_two = jnp.logical_not(row_first)[:, None] & jnp.logical_not(col_first)[None, :]
    selected = jnp.where(sub == 0, mask_one, mask_two)
    return jnp.where(selected, child_block, jnp.zeros((), jnp.float32))[None]


def solution(mesh):
    placed = (
        P(("groups", "row"), ("col", "sub")),
        P(("groups", "row"), ("col", "sub")),
        P("groups"),
    )
    return jax.shard_map(
        shards,
        mesh=mesh,
        in_specs=placed,
        out_specs=P("sub", ("groups", "row"), "col"),
        check_vma=False,
    )
```

profile of v0, /device:TPU:41, one launch (start us, length us, event | category | flops | bytes accessed | tf_op | source)
XLA Modules:
  0.0 284.6 jit_solution(17117127371487717278)
XLA Ops:
  7.3 2.1 reshape.32
  9.4 3.5 %fusion.14 = (f32[256,2,256]{2,1,0:T(2,128)S(1)}, f32[256,2,256]{2,1,0:T(2,128)S(1)}) fusion(pred[]{:T(512)S(6)} %eq.14, f32[256,2,2,256]{3,2,1,0:T(2,128)S(1)} %reshape.32), kind=kLoop, calls=%fused_computation.19 | loop fusion | flops 262144 | bytes 2097153 | tf_op jit(solution)/shard_map/jit(_where)/select_n | solution.py:46
  13.0 4.4 %collective-permute-start.1 = (f32[256,512]{1,0:T(8,128)S(1)}, f32[256,512]{1,0:T(8,128)S(1)}, u32[]{:S(2)}, u32[]{:S(2)}) collective-permute-start(f32[256,512]{1,0:T(8,128)S(1)} %bitcast.36), channel_id=1, source_target_pairs={{0,8},{8,0},{16,24},{24,16},{32,40},{40,32},{48,56},{56,48},{64,72... | collective-permute-start | bytes 1572872 | tf_op jit(solution)/shard_map/ppermute | solution.py:17
  17.5 11.6 %collective-permute-done.1 = f32[256,512]{1,0:T(8,128)S(1)} collective-permute-done((f32[256,512]{1,0:T(8,128)S(1)}, f32[256,512]{1,0:T(8,128)S(1)}, u32[]{:S(2)}, u32[]{:S(2)}) %collective-permute-start.1) | collective-permute-done | bytes 524320 | tf_op jit(solution)/shard_map/ppermute | solution.py:17
  29.2 3.3 %collective-permute-start.3 = (f32[512,512]{1,0:T(8,128)S(1)}, f32[512,512]{1,0:T(8,128)S(1)}, u32[]{:S(2)}, u32[]{:S(2)}) collective-permute-start(f32[512,512]{1,0:T(8,128)S(1)} %constant_dynamic-update-slice_fusion), channel_id=1, source_target_pairs={{0,2},{2,4},{4,6},{6,0},{1,3},{3,5},{5,7},{7,1},{8,10},{10,12},{12... | collective-permute-start | bytes 3145736 | tf_op jit(solution)/shard_map/ppermute | solution.py:12
  32.5 3.5 %collective-permute-start.6 = (f32[512,512]{1,0:T(8,128)S(1)}, f32[512,512]{1,0:T(8,128)S(1)}, u32[]{:S(2)}, u32[]{:S(2)}) collective-permute-start(f32[512,512]{1,0:T(8,128)S(1)} %constant_dynamic-update-slice_fusion), channel_id=1, source_target_pairs={{0,6},{2,0},{4,2},{6,4},{1,7},{3,1},{5,3},{7,5},{8,14},{10,8},{12,... | collective-permute-start | bytes 3145736 | tf_op jit(solution)/shard_map/ppermute | solution.py:12
  36.0 3.1 %collective-permute-start = (f32[256,128]{1,0:T(8,128)S(1)}, f32[256,128]{1,0:T(8,128)S(1)}, u32[]{:S(2)}, u32[]{:S(2)}) collective-permute-start(f32[256,128]{1,0:T(8,128)S(1)} %copy-done.5), channel_id=1, source_target_pairs={{0,8},{8,0},{16,24},{24,16},{32,40},{40,32},{48,56},{56,48},{64,72... | collective-permute-start | bytes 393224 | tf_op jit(solution)/shard_map/ppermute | solution.py:17
  39.1 30.1 %all-gather = f32[1024,128]{1,0:T(8,128)} all-gather(f32[128,128]{1,0:T(8,128)S(1)} %get-tuple-element.11), channel_id=2, replica_groups=mesh['groups'=2,'row'=32,'col'=4,'sub'=2] {'col','sub'}, dimensions={0}, use_global_device_ids=true | all-gather | bytes 589824 | tf_op jit(solution)/shard_map/all_gather | solution.py:29
  70.1 3.5 %collective-permute-start.5 = (f32[256,512]{1,0:T(8,128)}, f32[256,512]{1,0:T(8,128)}, u32[]{:S(2)}, u32[]{:S(2)}) collective-permute-start(f32[256,512]{1,0:T(8,128)} %slice.38), channel_id=1, source_target_pairs={{0,2},{2,4},{4,6},{6,0},{1,3},{3,5},{5,7},{7,1},{8,10},{10,12},{12... | collective-permute-start | bytes 1572872 | tf_op jit(solution)/shard_map/ppermute | solution.py:12
  73.6 23.2 %all-gather.1 = f32[1024,128]{1,0:T(8,128)} all-gather(f32[128,128]{1,0:T(8,128)S(1)} %get-tuple-element.12), channel_id=3, replica_groups=mesh['groups'=2,'row'=32,'col'=4,'sub'=2] {'col','sub'}, dimensions={0}, use_global_device_ids=true | all-gather | bytes 589824 | tf_op jit(solution)/shard_map/all_gather | solution.py:29
  101.0 3.4 %collective-permute-start.7 = (f32[256,512]{1,0:T(8,128)S(1)}, f32[256,512]{1,0:T(8,128)S(1)}, u32[]{:S(2)}, u32[]{:S(2)}) collective-permute-start(f32[256,512]{1,0:T(8,128)S(1)} %slice.39), channel_id=1, source_target_pairs={{0,6},{2,0},{4,2},{6,4},{1,7},{3,1},{5,3},{7,5},{8,14},{10,8},{12,... | collective-permute-start | bytes 1572872 | tf_op jit(solution)/shard_map/ppermute | solution.py:12
  104.4 21.8 %all-gather.2 = f32[1024,128]{1,0:T(8,128)} all-gather(f32[128,128]{1,0:T(8,128)S(1)} %get-tuple-element.13), channel_id=4, replica_groups=mesh['groups'=2,'row'=32,'col'=4,'sub'=2] {'col','sub'}, dimensions={0}, use_global_device_ids=true | all-gather | bytes 589824 | tf_op jit(solution)/shard_map/all_gather | solution.py:29
  131.0 2.3 collective-permute-start.8
  133.3 14.5 %all-gather.3 = f32[1024,128]{1,0:T(8,128)} all-gather(f32[128,128]{1,0:T(8,128)S(1)} %get-tuple-element.14), channel_id=5, replica_groups=mesh['groups'=2,'row'=32,'col'=4,'sub'=2] {'col','sub'}, dimensions={0}, use_global_device_ids=true | all-gather | bytes 589824 | tf_op jit(solution)/shard_map/all_gather | solution.py:29
  154.1 2.3 collective-permute-start.9
  158.5 2.3 fusion.20
  161.8 2.2 fusion.25
  164.0 2.2 fusion.18
  167.3 2.4 fusion.11
  169.7 2.2 fusion.8
  173.8 20.8 %all_to_all.10 = f32[4,8,32,128]{3,2,1,0:T(8,128)S(1)} all-to-all(f32[4,8,32,128]{3,2,1,0:T(8,128)S(1)} %bitcast.35), channel_id=1, replica_groups={{0,8,16,24},{32,40,48,56},{64,72,80,88},{96,104,112,120},{128,136,144,1..., dimensions={0} | all-to-all | bytes 1048576 | tf_op jit(solution)/shard_map/all_to_all | solution.py:73
  195.3 49.8 %all-to-all-start.1 = ((f32[8,32,128]{2,1,0:T(8,128)}), f32[8,32,128]{2,1,0:T(8,128)S(1)}, u32[]{:S(2)}, u32[]{:S(2)}) async-start(f32[8,32,128]{2,1,0:T(8,128)} %reduce_sum.18), calls=%async_computation.1 | async-start | bytes 262144 | tf_op jit(solution)/shard_map/all_to_all | solution.py:74
  245.8 23.3 %all-to-all-done.1 = f32[8,32,128]{2,1,0:T(8,128)S(1)} async-done(((f32[8,32,128]{2,1,0:T(8,128)}), f32[8,32,128]{2,1,0:T(8,128)S(1)}, u32[]{:S(2)}, u32[]{:S(2)}) %all-to-all-start.1) | async-done | bytes 131104 | tf_op jit(solution)/shard_map/all_to_all | solution.py:74
  269.1 8.0 %all_gather.39 = f32[32,256]{1,0:T(8,128)S(1)} all-gather(f32[32,128]{1,0:T(8,128)S(1)} %reduce_sum.19), channel_id=1, replica_groups=mesh['groups'=2,'row'=32,'col'=4,'sub'=2] {'sub'}, dimensions={1}, use_global_device_ids=true | all-gather | bytes 49152 | tf_op jit(solution)/shard_map/all_gather | solution.py:77
  (50 shorter events, 24.3 us)
Async XLA Ops:
  6.5 149.8 %all-gather.6.cloned.1.call-start = ((), (), s32[]{:S(2)}) async-start(), calls=%async_computation.2 | async-start | bytes 2228224 | tf_op jit(solution)/shard_map/all_gather | solution.py:43
  13.0 23.0 %copy-start.5 = (f32[256,128]{1,0:T(8,128)S(1)}, f32[256,128]{1,0:T(8,128)}, u32[]{:S(2)}) copy-start(f32[256,128]{1,0:T(8,128)} %param.4) | copy-start | bytes 393220
  13.0 16.1 %collective-permute-start.1 = (f32[256,512]{1,0:T(8,128)S(1)}, f32[256,512]{1,0:T(8,128)S(1)}, u32[]{:S(2)}, u32[]{:S(2)}) collective-permute-start(f32[256,512]{1,0:T(8,128)S(1)} %bitcast.36), channel_id=1, source_target_pairs={{0,8},{8,0},{16,24},{24,16},{32,40},{40,32},{48,56},{56,48},{64,72... | collective-permute-start | bytes 1572872 | tf_op jit(solution)/shard_map/ppermute | solution.py:17
  29.2 40.1 %collective-permute-start.3 = (f32[512,512]{1,0:T(8,128)S(1)}, f32[512,512]{1,0:T(8,128)S(1)}, u32[]{:S(2)}, u32[]{:S(2)}) collective-permute-start(f32[512,512]{1,0:T(8,128)S(1)} %constant_dynamic-update-slice_fusion), channel_id=1, source_target_pairs={{0,2},{2,4},{4,6},{6,0},{1,3},{3,5},{5,7},{7,1},{8,10},{10,12},{12... | collective-permute-start | bytes 3145736 | tf_op jit(solution)/shard_map/ppermute | solution.py:12
  32.5 68.5 %collective-permute-start.6 = (f32[512,512]{1,0:T(8,128)S(1)}, f32[512,512]{1,0:T(8,128)S(1)}, u32[]{:S(2)}, u32[]{:S(2)}) collective-permute-start(f32[512,512]{1,0:T(8,128)S(1)} %constant_dynamic-update-slice_fusion), channel_id=1, source_target_pairs={{0,6},{2,0},{4,2},{6,4},{1,7},{3,1},{5,3},{7,5},{8,14},{10,8},{12,... | collective-permute-start | bytes 3145736 | tf_op jit(solution)/shard_map/ppermute | solution.py:12
  36.0 68.4 %collective-permute-start = (f32[256,128]{1,0:T(8,128)S(1)}, f32[256,128]{1,0:T(8,128)S(1)}, u32[]{:S(2)}, u32[]{:S(2)}) collective-permute-start(f32[256,128]{1,0:T(8,128)S(1)} %copy-done.5), channel_id=1, source_target_pairs={{0,8},{8,0},{16,24},{24,16},{32,40},{40,32},{48,56},{56,48},{64,72... | collective-permute-start | bytes 393224 | tf_op jit(solution)/shard_map/ppermute | solution.py:17
  70.1 58.2 %collective-permute-start.5 = (f32[256,512]{1,0:T(8,128)}, f32[256,512]{1,0:T(8,128)}, u32[]{:S(2)}, u32[]{:S(2)}) collective-permute-start(f32[256,512]{1,0:T(8,128)} %slice.38), channel_id=1, source_target_pairs={{0,2},{2,4},{4,6},{6,0},{1,3},{3,5},{5,7},{7,1},{8,10},{10,12},{12... | collective-permute-start | bytes 1572872 | tf_op jit(solution)/shard_map/ppermute | solution.py:12
  101.0 29.2 %collective-permute-start.7 = (f32[256,512]{1,0:T(8,128)S(1)}, f32[256,512]{1,0:T(8,128)S(1)}, u32[]{:S(2)}, u32[]{:S(2)}) collective-permute-start(f32[256,512]{1,0:T(8,128)S(1)} %slice.39), channel_id=1, source_target_pairs={{0,6},{2,0},{4,2},{6,4},{1,7},{3,1},{5,3},{7,5},{8,14},{10,8},{12,... | collective-permute-start | bytes 1572872 | tf_op jit(solution)/shard_map/ppermute | solution.py:12
  126.2 35.6 %collective-permute-start.2 = (f32[512,512]{1,0:T(8,128)S(1)}, f32[512,512]{1,0:T(8,128)}, u32[]{:S(2)}, u32[]{:S(2)}) collective-permute-start(f32[512,512]{1,0:T(8,128)S(1)} %constant_dynamic-update-slice_fusion), channel_id=1, source_target_pairs={{0,1},{1,0},{2,3},{3,2},{4,5},{5,4},{6,7},{7,6},{8,9},{9,8},{10,11... | collective-permute-start | bytes 3145736 | tf_op jit(solution)/shard_map/ppermute | solution.py:17
  131.0 33.0 %collective-permute-start.8 = (f32[512,512]{1,0:T(8,128)}, f32[512,512]{1,0:T(8,128)}, u32[]{:S(2)}, u32[]{:S(2)}) collective-permute-start(f32[512,512]{1,0:T(8,128)} %constant_dynamic-update-slice_fusion.2), channel_id=1, source_target_pairs={{0,1},{1,0},{2,3},{3,2},{4,5},{5,4},{6,7},{7,6},{8,9},{9,8},{10,11... | collective-permute-start | bytes 3145736 | tf_op jit(solution)/shard_map/ppermute | solution.py:17
  152.0 15.3 %collective-permute-start.4 = (f32[512,512]{1,0:T(8,128)S(1)}, f32[512,512]{1,0:T(8,128)}, u32[]{:S(2)}, u32[]{:S(2)}) collective-permute-start(f32[512,512]{1,0:T(8,128)S(1)} %collective-permute-done.3), channel_id=1, source_target_pairs={{0,1},{1,0},{2,3},{3,2},{4,5},{5,4},{6,7},{7,6},{8,9},{9,8},{10,11... | collective-permute-start | bytes 3145736 | tf_op jit(solution)/shard_map/ppermute | solution.py:17
  154.1 15.6 %collective-permute-start.9 = (f32[512,512]{1,0:T(8,128)S(1)}, f32[512,512]{1,0:T(8,128)}, u32[]{:S(2)}, u32[]{:S(2)}) collective-permute-start(f32[512,512]{1,0:T(8,128)S(1)} %collective-permute-done.6), channel_id=1, source_target_pairs={{0,1},{1,0},{2,3},{3,2},{4,5},{5,4},{6,7},{7,6},{8,9},{9,8},{10,11... | collective-permute-start | bytes 3145736 | tf_op jit(solution)/shard_map/ppermute | solution.py:17
  156.4 4.4 %copy-start = (f32[4096,128]{1,0:T(8,128)S(1)}, f32[4096,128]{1,0:T(8,128)}, u32[]{:S(2)}) copy-start(f32[4096,128]{1,0:T(8,128)} %all-gather.6.cloned.1.call-done) | copy-start | bytes 6291460
  167.2 4.7 %copy-start.1 = (f32[8,128,128]{1,2,0:T(8,128)S(1)}, f32[8,128,128]{1,2,0:T(8,128)}, u32[]{:S(2)}) copy-start(f32[8,128,128]{1,2,0:T(8,128)} %copy.13) | copy-start | bytes 1572868
  167.2 4.7 %copy-start.2 = (f32[8,128,128]{1,2,0:T(8,128)S(1)}, f32[8,128,128]{1,2,0:T(8,128)}, u32[]{:S(2)}) copy-start(f32[8,128,128]{1,2,0:T(8,128)} %copy.14) | copy-start | bytes 1572868
  167.3 4.7 %copy-start.3 = (f32[8,128,128]{1,2,0:T(8,128)S(1)}, f32[8,128,128]{1,2,0:T(8,128)}, u32[]{:S(2)}) copy-start(f32[8,128,128]{1,2,0:T(8,128)} %copy.15) | copy-start | bytes 1572868
  167.3 4.7 %copy-start.4 = (f32[8,128,128]{1,2,0:T(8,128)S(1)}, f32[8,128,128]{1,2,0:T(8,128)}, u32[]{:S(2)}) copy-start(f32[8,128,128]{1,2,0:T(8,128)} %copy.16) | copy-start | bytes 1572868
  195.3 73.8 %all-to-all-start.1 = ((f32[8,32,128]{2,1,0:T(8,128)}), f32[8,32,128]{2,1,0:T(8,128)S(1)}, u32[]{:S(2)}, u32[]{:S(2)}) async-start(f32[8,32,128]{2,1,0:T(8,128)} %reduce_sum.18), calls=%async_computation.1 | async-start | bytes 262144 | tf_op jit(solution)/shard_map/all_to_all | solution.py:74
Sparse Core Ops, SparseCore 0:
  9.4 122.9 all-gather.5
where the time goes:
time: 286 us; the launch traced here: 285 us
  blocking collectives  119 us (42%)
  starting transfers between devices  79.8 us (28%)
  waiting for transfers between devices  35.7 us (12%)
  matrix products  17.1 us (6%)
  between operations  14.5 us (5%)
  local copies, waits for them, and re-layouts  14.2 us (5%)
  other arithmetic  4.92 us (2%)
    all_gather x4, blocking collectives, all_columns(): lax.all_gather(basis[i * half:(i + 1) * half], ('col', 'sub'), axis=0)  89.7 us
    all_to_all x1, starting transfers between devices, shards(): lax.all_to_all(partial, 'row', 0, 0, tiled=True, axis_index_groups=far_gr...  49.8 us
    all_to_all x1, waiting for transfers between devices, shards(): lax.all_to_all(partial, 'row', 0, 0, tiled=True, axis_index_groups=far_gr...  23.3 us
    all_to_all x1, blocking collectives, shards(): lax.all_to_all(partial, 'row', 0, 0, tiled=True, axis_index_groups=near_g...  20.8 us
    dot_general x9, matrix products, product(): lax.dot_general(left, right, (contract, ((), ())), precision=PRECISION, p...  17.1 us
    ppermute x6, starting transfers between devices, swapped(): return lax.ppermute(array, axis, [(i, i ^ 1) for i in range(size)])  16.3 us
    ppermute x4, starting transfers between devices, shifted(): lax.ppermute(array, axis, [(i, (i + step) % size) for i in range(size)])  13.7 us
    ppermute x6, waiting for transfers between devices, swapped(): return lax.ppermute(array, axis, [(i, i ^ 1) for i in range(size)])  11.6 us
  transfers between devices with their start and end apart: 12, of which 2 were waited for; matrix products, arithmetic and copies ran while one was open for 11% of the time, Pallas kernels for 0%

commit v1 on v0

--- a/solution.py
+++ b/solution.py
@@ -74,7 +74,10 @@
     proj_block = lax.all_to_all(partial, "row", 0, 0, tiled=True, axis_index_groups=far_groups).sum(
         0
     )
-    child_block = lax.all_gather(proj_block, "sub", axis=1, tiled=True)
+    count = lax.axis_size("sub")
+    terms = jnp.stack([proj_block for _ in range(count)])
+    terms = lax.all_to_all(terms, "sub", split_axis=0, concat_axis=0)
+    child_block = jnp.concatenate(terms, axis=1)
     row_ids = jnp.arange(child_block.shape[0], dtype=jnp.int32) + row * child_block.shape[0]
     col_ids = jnp.arange(child_block.shape[1], dtype=jnp.int32) + col * child_block.shape[1]
     leading = split_size[0]

time: 286 us -> 288 us (level)
    all_to_all x0 -> x1, blocking collectives: none -> 9.88 us  [shards(): terms = lax.all_to_all(terms, 'sub', split_axis=0, concat_axis=0)]
    all_gather x1 -> x0, blocking collectives: 7.99 us -> none  [shards(): child_block = lax.all_gather(proj_block, 'sub', axis=1, tiled=True)]
where the time goes in v1:
time: 288 us; the launch traced here: 287 us
  blocking collectives  120 us (42%)
  starting transfers between devices  79.8 us (28%)
  waiting for transfers between devices  35.7 us (12%)
  matrix products  17.1 us (6%)
  between operations  14.5 us (5%)
  local copies, waits for them, and re-layouts  14.2 us (5%)
  other arithmetic  4.93 us (2%)
    all_gather x4, blocking collectives, all_columns(): lax.all_gather(basis[i * half:(i + 1) * half], ('col', 'sub'), axis=0)  89.7 us
    all_to_all x1, starting transfers between devices, shards(): lax.all_to_all(partial, 'row', 0, 0, tiled=True, axis_index_groups=far_gr...  49.8 us
    all_to_all x1, waiting for transfers between devices, shards(): lax.all_to_all(partial, 'row', 0, 0, tiled=True, axis_index_groups=far_gr...  23.3 us
    all_to_all x1, blocking collectives, shards(): lax.all_to_all(partial, 'row', 0, 0, tiled=True, axis_index_groups=near_g...  20.8 us
    dot_general x9, matrix products, product(): lax.dot_general(left, right, (contract, ((), ())), precision=PRECISION, p...  17.1 us
    ppermute x6, starting transfers between devices, swapped(): return lax.ppermute(array, axis, [(i, i ^ 1) for i in range(size)])  16.3 us
    ppermute x4, starting transfers between devices, shifted(): lax.ppermute(array, axis, [(i, (i + step) % size) for i in range(size)])  13.7 us
    ppermute x6, waiting for transfers between devices, swapped(): return lax.ppermute(array, axis, [(i, i ^ 1) for i in range(size)])  11.6 us
  transfers between devices with their start and end apart: 12, of which 2 were waited for; matrix products, arithmetic and copies ran while one was open for 11% of the time, Pallas kernels for 0%

profile of v1, /device:TPU:41, one launch (start us, length us, event | category | flops | bytes accessed | tf_op | source)
XLA Modules:
  0.0 286.6 jit_solution(5933895443143171713)
XLA Ops:
  7.3 2.1 reshape.137
  9.4 3.5 %fusion.14 = (f32[256,2,256]{2,1,0:T(2,128)S(1)}, f32[256,2,256]{2,1,0:T(2,128)S(1)}) fusion(pred[]{:T(512)S(6)} %eq.14, f32[256,2,2,256]{3,2,1,0:T(2,128)S(1)} %reshape.137), kind=kLoop, calls=%fused_computation.19 | loop fusion | flops 262144 | bytes 2097153 | tf_op jit(solution)/shard_map/jit(_where)/select_n | solution.py:46
  13.0 4.4 %collective-permute-start.1 = (f32[256,512]{1,0:T(8,128)S(1)}, f32[256,512]{1,0:T(8,128)S(1)}, u32[]{:S(2)}, u32[]{:S(2)}) collective-permute-start(f32[256,512]{1,0:T(8,128)S(1)} %bitcast.36), channel_id=1, source_target_pairs={{0,8},{8,0},{16,24},{24,16},{32,40},{40,32},{48,56},{56,48},{64,72... | collective-permute-start | bytes 1572872 | tf_op jit(solution)/shard_map/ppermute | solution.py:17
  17.5 11.6 %collective-permute-done.1 = f32[256,512]{1,0:T(8,128)S(1)} collective-permute-done((f32[256,512]{1,0:T(8,128)S(1)}, f32[256,512]{1,0:T(8,128)S(1)}, u32[]{:S(2)}, u32[]{:S(2)}) %collective-permute-start.1) | collective-permute-done | bytes 524320 | tf_op jit(solution)/shard_map/ppermute | solution.py:17
  29.2 3.3 %collective-permute-start.3 = (f32[512,512]{1,0:T(8,128)S(1)}, f32[512,512]{1,0:T(8,128)S(1)}, u32[]{:S(2)}, u32[]{:S(2)}) collective-permute-start(f32[512,512]{1,0:T(8,128)S(1)} %constant_dynamic-update-slice_fusion), channel_id=1, source_target_pairs={{0,2},{2,4},{4,6},{6,0},{1,3},{3,5},{5,7},{7,1},{8,10},{10,12},{12... | collective-permute-start | bytes 3145736 | tf_op jit(solution)/shard_map/ppermute | solution.py:12
  32.5 3.5 %collective-permute-start.6 = (f32[512,512]{1,0:T(8,128)S(1)}, f32[512,512]{1,0:T(8,128)S(1)}, u32[]{:S(2)}, u32[]{:S(2)}) collective-permute-start(f32[512,512]{1,0:T(8,128)S(1)} %constant_dynamic-update-slice_fusion), channel_id=1, source_target_pairs={{0,6},{2,0},{4,2},{6,4},{1,7},{3,1},{5,3},{7,5},{8,14},{10,8},{12,... | collective-permute-start | bytes 3145736 | tf_op jit(solution)/shard_map/ppermute | solution.py:12
  36.0 3.1 %collective-permute-start = (f32[256,128]{1,0:T(8,128)S(1)}, f32[256,128]{1,0:T(8,128)S(1)}, u32[]{:S(2)}, u32[]{:S(2)}) collective-permute-start(f32[256,128]{1,0:T(8,128)S(1)} %copy-done.5), channel_id=1, source_target_pairs={{0,8},{8,0},{16,24},{24,16},{32,40},{40,32},{48,56},{56,48},{64,72... | collective-permute-start | bytes 393224 | tf_op jit(solution)/shard_map/ppermute | solution.py:17
  39.1 30.1 %all-gather = f32[1024,128]{1,0:T(8,128)} all-gather(f32[128,128]{1,0:T(8,128)S(1)} %get-tuple-element.11), channel_id=2, replica_groups=mesh['groups'=2,'row'=32,'col'=4,'sub'=2] {'col','sub'}, dimensions={0}, use_global_device_ids=true | all-gather | bytes 589824 | tf_op jit(solution)/shard_map/all_gather | solution.py:29
  70.1 3.5 %collective-permute-start.5 = (f32[256,512]{1,0:T(8,128)}, f32[256,512]{1,0:T(8,128)}, u32[]{:S(2)}, u32[]{:S(2)}) collective-permute-start(f32[256,512]{1,0:T(8,128)} %slice.38), channel_id=1, source_target_pairs={{0,2},{2,4},{4,6},{6,0},{1,3},{3,5},{5,7},{7,1},{8,10},{10,12},{12... | collective-permute-start | bytes 1572872 | tf_op jit(solution)/shard_map/ppermute | solution.py:12
  73.6 23.2 %all-gather.1 = f32[1024,128]{1,0:T(8,128)} all-gather(f32[128,128]{1,0:T(8,128)S(1)} %get-tuple-element.12), channel_id=3, replica_groups=mesh['groups'=2,'row'=32,'col'=4,'sub'=2] {'col','sub'}, dimensions={0}, use_global_device_ids=true | all-gather | bytes 589824 | tf_op jit(solution)/shard_map/all_gather | solution.py:29
  101.0 3.4 %collective-permute-start.7 = (f32[256,512]{1,0:T(8,128)S(1)}, f32[256,512]{1,0:T(8,128)S(1)}, u32[]{:S(2)}, u32[]{:S(2)}) collective-permute-start(f32[256,512]{1,0:T(8,128)S(1)} %slice.39), channel_id=1, source_target_pairs={{0,6},{2,0},{4,2},{6,4},{1,7},{3,1},{5,3},{7,5},{8,14},{10,8},{12,... | collective-permute-start | bytes 1572872 | tf_op jit(solution)/shard_map/ppermute | solution.py:12
  104.4 21.8 %all-gather.2 = f32[1024,128]{1,0:T(8,128)} all-gather(f32[128,128]{1,0:T(8,128)S(1)} %get-tuple-element.13), channel_id=4, replica_groups=mesh['groups'=2,'row'=32,'col'=4,'sub'=2] {'col','sub'}, dimensions={0}, use_global_device_ids=true | all-gather | bytes 589824 | tf_op jit(solution)/shard_map/all_gather | solution.py:29
  131.0 2.3 collective-permute-start.8
  133.3 14.5 %all-gather.3 = f32[1024,128]{1,0:T(8,128)} all-gather(f32[128,128]{1,0:T(8,128)S(1)} %get-tuple-element.14), channel_id=5, replica_groups=mesh['groups'=2,'row'=32,'col'=4,'sub'=2] {'col','sub'}, dimensions={0}, use_global_device_ids=true | all-gather | bytes 589824 | tf_op jit(solution)/shard_map/all_gather | solution.py:29
  154.1 2.3 collective-permute-start.9
  158.5 2.3 fusion.20
  161.8 2.2 fusion.25
  164.0 2.2 fusion.18
  167.3 2.4 fusion.11
  169.7 2.2 fusion.8
  173.8 20.8 %all_to_all.15 = f32[4,8,32,128]{3,2,1,0:T(8,128)S(1)} all-to-all(f32[4,8,32,128]{3,2,1,0:T(8,128)S(1)} %bitcast.35), channel_id=1, replica_groups={{0,8,16,24},{32,40,48,56},{64,72,80,88},{96,104,112,120},{128,136,144,1..., dimensions={0} | all-to-all | bytes 1048576 | tf_op jit(solution)/shard_map/all_to_all | solution.py:73
  195.3 49.8 %all-to-all-start.1 = ((f32[8,32,128]{2,1,0:T(8,128)}), f32[8,32,128]{2,1,0:T(8,128)S(1)}, u32[]{:S(2)}, u32[]{:S(2)}) async-start(f32[8,32,128]{2,1,0:T(8,128)} %reduce_sum.18), calls=%async_computation.1 | async-start | bytes 262144 | tf_op jit(solution)/shard_map/all_to_all | solution.py:74
  245.8 23.3 %all-to-all-done.1 = f32[8,32,128]{2,1,0:T(8,128)S(1)} async-done(((f32[8,32,128]{2,1,0:T(8,128)}), f32[8,32,128]{2,1,0:T(8,128)S(1)}, u32[]{:S(2)}, u32[]{:S(2)}) %all-to-all-start.1) | async-done | bytes 131104 | tf_op jit(solution)/shard_map/all_to_all | solution.py:74
  269.1 9.9 %all_to_all.16 = f32[2,32,128]{2,1,0:T(8,128)S(1)} all-to-all(f32[2,32,128]{2,1,0:T(8,128)S(1)} %pad_maximum_fusion), channel_id=1, replica_groups=mesh['groups'=2,'row'=32,'col'=4,'sub'=2] {'sub'}, dimensions={0} | all-to-all | bytes 65536 | tf_op jit(solution)/shard_map/all_to_all | solution.py:79
  (53 shorter events, 24.4 us)
Async XLA Ops:
  6.5 149.8 %all-gather.6.cloned.1.call-start = ((), (), s32[]{:S(2)}) async-start(), calls=%async_computation.3 | async-start | bytes 2228224 | tf_op jit(solution)/shard_map/all_gather | solution.py:43
  13.0 23.0 %copy-start.5 = (f32[256,128]{1,0:T(8,128)S(1)}, f32[256,128]{1,0:T(8,128)}, u32[]{:S(2)}) copy-start(f32[256,128]{1,0:T(8,128)} %param.4) | copy-start | bytes 393220
  13.0 16.1 %collective-permute-start.1 = (f32[256,512]{1,0:T(8,128)S(1)}, f32[256,512]{1,0:T(8,128)S(1)}, u32[]{:S(2)}, u32[]{:S(2)}) collective-permute-start(f32[256,512]{1,0:T(8,128)S(1)} %bitcast.36), channel_id=1, source_target_pairs={{0,8},{8,0},{16,24},{24,16},{32,40},{40,32},{48,56},{56,48},{64,72... | collective-permute-start | bytes 1572872 | tf_op jit(solution)/shard_map/ppermute | solution.py:17
  29.2 40.1 %collective-permute-start.3 = (f32[512,512]{1,0:T(8,128)S(1)}, f32[512,512]{1,0:T(8,128)S(1)}, u32[]{:S(2)}, u32[]{:S(2)}) collective-permute-start(f32[512,512]{1,0:T(8,128)S(1)} %constant_dynamic-update-slice_fusion), channel_id=1, source_target_pairs={{0,2},{2,4},{4,6},{6,0},{1,3},{3,5},{5,7},{7,1},{8,10},{10,12},{12... | collective-permute-start | bytes 3145736 | tf_op jit(solution)/shard_map/ppermute | solution.py:12
  32.5 68.5 %collective-permute-start.6 = (f32[512,512]{1,0:T(8,128)S(1)}, f32[512,512]{1,0:T(8,128)S(1)}, u32[]{:S(2)}, u32[]{:S(2)}) collective-permute-start(f32[512,512]{1,0:T(8,128)S(1)} %constant_dynamic-update-slice_fusion), channel_id=1, source_target_pairs={{0,6},{2,0},{4,2},{6,4},{1,7},{3,1},{5,3},{7,5},{8,14},{10,8},{12,... | collective-permute-start | bytes 3145736 | tf_op jit(solution)/shard_map/ppermute | solution.py:12
  36.0 68.4 %collective-permute-start = (f32[256,128]{1,0:T(8,128)S(1)}, f32[256,128]{1,0:T(8,128)S(1)}, u32[]{:S(2)}, u32[]{:S(2)}) collective-permute-start(f32[256,128]{1,0:T(8,128)S(1)} %copy-done.5), channel_id=1, source_target_pairs={{0,8},{8,0},{16,24},{24,16},{32,40},{40,32},{48,56},{56,48},{64,72... | collective-permute-start | bytes 393224 | tf_op jit(solution)/shard_map/ppermute | solution.py:17
  70.1 58.2 %collective-permute-start.5 = (f32[256,512]{1,0:T(8,128)}, f32[256,512]{1,0:T(8,128)}, u32[]{:S(2)}, u32[]{:S(2)}) collective-permute-start(f32[256,512]{1,0:T(8,128)} %slice.38), channel_id=1, source_target_pairs={{0,2},{2,4},{4,6},{6,0},{1,3},{3,5},{5,7},{7,1},{8,10},{10,12},{12... | collective-permute-start | bytes 1572872 | tf_op jit(solution)/shard_map/ppermute | solution.py:12
  101.0 29.2 %collective-permute-start.7 = (f32[256,512]{1,0:T(8,128)S(1)}, f32[256,512]{1,0:T(8,128)S(1)}, u32[]{:S(2)}, u32[]{:S(2)}) collective-permute-start(f32[256,512]{1,0:T(8,128)S(1)} %slice.39), channel_id=1, source_target_pairs={{0,6},{2,0},{4,2},{6,4},{1,7},{3,1},{5,3},{7,5},{8,14},{10,8},{12,... | collective-permute-start | bytes 1572872 | tf_op jit(solution)/shard_map/ppermute | solution.py:12
  126.2 35.6 %collective-permute-start.2 = (f32[512,512]{1,0:T(8,128)S(1)}, f32[512,512]{1,0:T(8,128)}, u32[]{:S(2)}, u32[]{:S(2)}) collective-permute-start(f32[512,512]{1,0:T(8,128)S(1)} %constant_dynamic-update-slice_fusion), channel_id=1, source_target_pairs={{0,1},{1,0},{2,3},{3,2},{4,5},{5,4},{6,7},{7,6},{8,9},{9,8},{10,11... | collective-permute-start | bytes 3145736 | tf_op jit(solution)/shard_map/ppermute | solution.py:17
  131.0 33.0 %collective-permute-start.8 = (f32[512,512]{1,0:T(8,128)}, f32[512,512]{1,0:T(8,128)}, u32[]{:S(2)}, u32[]{:S(2)}) collective-permute-start(f32[512,512]{1,0:T(8,128)} %constant_dynamic-update-slice_fusion.2), channel_id=1, source_target_pairs={{0,1},{1,0},{2,3},{3,2},{4,5},{5,4},{6,7},{7,6},{8,9},{9,8},{10,11... | collective-permute-start | bytes 3145736 | tf_op jit(solution)/shard_map/ppermute | solution.py:17
  152.0 15.3 %collective-permute-start.4 = (f32[512,512]{1,0:T(8,128)S(1)}, f32[512,512]{1,0:T(8,128)}, u32[]{:S(2)}, u32[]{:S(2)}) collective-permute-start(f32[512,512]{1,0:T(8,128)S(1)} %collective-permute-done.3), channel_id=1, source_target_pairs={{0,1},{1,0},{2,3},{3,2},{4,5},{5,4},{6,7},{7,6},{8,9},{9,8},{10,11... | collective-permute-start | bytes 3145736 | tf_op jit(solution)/shard_map/ppermute | solution.py:17
  154.1 15.6 %collective-permute-start.9 = (f32[512,512]{1,0:T(8,128)S(1)}, f32[512,512]{1,0:T(8,128)}, u32[]{:S(2)}, u32[]{:S(2)}) collective-permute-start(f32[512,512]{1,0:T(8,128)S(1)} %collective-permute-done.6), channel_id=1, source_target_pairs={{0,1},{1,0},{2,3},{3,2},{4,5},{5,4},{6,7},{7,6},{8,9},{9,8},{10,11... | collective-permute-start | bytes 3145736 | tf_op jit(solution)/shard_map/ppermute | solution.py:17
  156.4 4.4 %copy-start = (f32[4096,128]{1,0:T(8,128)S(1)}, f32[4096,128]{1,0:T(8,128)}, u32[]{:S(2)}) copy-start(f32[4096,128]{1,0:T(8,128)} %all-gather.6.cloned.1.call-done) | copy-start | bytes 6291460
  167.2 4.7 %copy-start.1 = (f32[8,128,128]{1,2,0:T(8,128)S(1)}, f32[8,128,128]{1,2,0:T(8,128)}, u32[]{:S(2)}) copy-start(f32[8,128,128]{1,2,0:T(8,128)} %copy.19) | copy-start | bytes 1572868
  167.2 4.7 %copy-start.2 = (f32[8,128,128]{1,2,0:T(8,128)S(1)}, f32[8,128,128]{1,2,0:T(8,128)}, u32[]{:S(2)}) copy-start(f32[8,128,128]{1,2,0:T(8,128)} %copy.20) | copy-start | bytes 1572868
  167.3 4.7 %copy-start.3 = (f32[8,128,128]{1,2,0:T(8,128)S(1)}, f32[8,128,128]{1,2,0:T(8,128)}, u32[]{:S(2)}) copy-start(f32[8,128,128]{1,2,0:T(8,128)} %copy.21) | copy-start | bytes 1572868
  167.3 4.7 %copy-start.4 = (f32[8,128,128]{1,2,0:T(8,128)S(1)}, f32[8,128,128]{1,2,0:T(8,128)}, u32[]{:S(2)}) copy-start(f32[8,128,128]{1,2,0:T(8,128)} %copy.22) | copy-start | bytes 1572868
  195.3 73.8 %all-to-all-start.1 = ((f32[8,32,128]{2,1,0:T(8,128)}), f32[8,32,128]{2,1,0:T(8,128)S(1)}, u32[]{:S(2)}, u32[]{:S(2)}) async-start(f32[8,32,128]{2,1,0:T(8,128)} %reduce_sum.18), calls=%async_computation.1 | async-start | bytes 262144 | tf_op jit(solution)/shard_map/all_to_all | solution.py:74
Sparse Core Ops, SparseCore 0:
  9.4 122.9 all-gather.5
